TPU v7x, 32 devices: a whole 2x2x4 slice. The times are simulated.
32 devices in a mesh: batch: 4 (over x, core), seq: 8 (over z, y).
Axes of the slice: x: 2, y: 2, z: 4, core: 2. Of those that a mesh axis runs over, the one named last changes fastest.
Arguments:
- tokens: bfloat16 [16, 2048, 768], P('batch', 'seq'), may hold values from -6 to 6
- prompts: float32 [50, 768], replicated, may hold values from -6 to 6
- image_id: int32 [16, 2048], P('batch'), may hold values from 0 to 8, as said below
- prompt_slot: int32 [16, 2048], P('batch', 'seq'), may hold values from 0 to 50, as said below
- ln1_gain: float32 [768], replicated, may hold values from 0.5 to 1.5
- ln1_bias: float32 [768], replicated, may hold values from -1.8 to 1.8
- w_qkv: bfloat16 [768, 2304], replicated, may hold values from -0.21875 to 0.21875
- bias_qv: float32 [1536], replicated, may hold values from -1.8 to 1.8
- w_out: bfloat16 [768, 768], replicated, may hold values from -0.875 to 0.875
- bias_out: float32 [768], replicated, may hold values from -1.8 to 1.8
- ln2_gain: float32 [768], replicated, may hold values from 0.5 to 1.5
- ln2_bias: float32 [768], replicated, may hold values from -1.8 to 1.8
- w_up: bfloat16 [768, 3072], replicated, may hold values from -0.21875 to 0.21875
- bias_up: float32 [3072], replicated, may hold values from -1.8 to 1.8
- w_down: bfloat16 [3072, 768], replicated, may hold values from -0.109375 to 0.109375
- bias_down: float32 [768], replicated, may hold values from -1.8 to 1.8
- cotangent: bfloat16 [16, 2048, 768], P('batch', 'seq'), may hold values from -6 to 6
Outputs:
- output: bfloat16 [16, 2048, 768], P('batch', 'seq')
- token_gradient: bfloat16 [16, 2048, 768], P('batch', 'seq')
- prompt_gradient: float32 [50, 768], replicated
Inputs may be any that keep to these rules, and one draw needn't show every extreme that they name: `image_id`: each row holds 8 runs of 247 consecutive positions with ids 0 to 7 in order; all other positions (padding, some before, between or after the runs) have id 8. `prompt_slot`: within each run of image_id, the first position is the class token, the next 50 carry slots 0 to 49 in order; class tokens, patches and padding carry 50.
All inputs are finite; a program needn't handle non-finite values.
Results may differ from a plain program's by a relative error of at most 0.012.
Values may be sent and summed in bfloat16 or wider, within the bound.
A program may use at most 384 MiB of HBM per device.

v0:
```python
import jax
import jax.numpy as jnp
from jax import lax
from jax.sharding import PartitionSpec as P

ATTENTION_HEADS = 12
HEAD_FEATURES = 64
PROMPTS = 50
IMAGES_PER_ROW = 8
IMAGE_TOKENS = 247


def passed_along(block, axis, distance):
    devices = range(lax.axis_size(axis))
    route = [(i - distance, i) for i in devices if i - distance in devices]
    return lax.ppermute(block, axis, route)


def normalize(value_rows):
    mean = jnp.mean(value_rows, axis=-1, keepdims=True)
    centered = value_rows - mean
    inverse = lax.rsqrt(jnp.mean(centered * centered, axis=-1, keepdims=True) + 1e-06)
    return (centered * inverse, inverse)


def norm_back(grad_in, normal_draws, inverse, gain):
    scaled = grad_in * gain
    return inverse * (
        scaled
        - jnp.mean(scaled, axis=-1, keepdims=True)
        - normal_draws * jnp.mean(scaled * normal_draws, axis=-1, keepdims=True)
    )


def block_rows(rows, span):
    group = min(rows, max(1, 512 // span))
    while rows % group:
        group = group - 1
    return group


def masked_scores(query_rows, key_rows, query_ids, key_ids, own_pos, key_pos):
    scores = jnp.einsum(
        "gqhd,gkhd->ghqk", query_rows, key_rows, preferred_element_type=jnp.float32
    ) * HEAD_FEATURES ** (-0.5)
    same_image = (query_ids[:, :, None] == key_ids[:, None, :]) & (query_ids < IMAGES_PER_ROW)[
        :, :, None
    ]
    permitted_mask = same_image | (own_pos[:, None] == key_pos[None, :])[None]
    return jnp.where(permitted_mask[:, None], scores, -1e30)


def body(
    tokens,
    prompts,
    image_id,
    prompt_slot,
    ln1_gain,
    ln1_bias,
    w_qkv,
    bias_qv,
    w_out,
    bias_out,
    ln2_gain,
    ln2_bias,
    w_up,
    bias_up,
    w_down,
    bias_down,
    cotangent,
):
    rows, span, width = tokens.shape
    length = image_id.shape[1]
    start = lax.axis_index("seq") * span
    own_ids = lax.dynamic_slice_in_dim(image_id, start, span, 1)
    own_pos = start + jnp.arange(span, dtype=jnp.int32)
    valid = (own_ids < IMAGES_PER_ROW).astype(jnp.float32)
    one_hot = (prompt_slot[..., None] == jnp.arange(PROMPTS, dtype=jnp.int32)).astype(jnp.float32)
    placed = jnp.einsum("rsn,nd->rsd", one_hot, prompts, precision=lax.Precision.HIGHEST)
    is_prompt = (prompt_slot < PROMPTS)[..., None]
    inserted = jnp.where(is_prompt, placed, tokens.astype(jnp.float32))
    normal1, inverse1 = normalize(inserted)
    normed1 = (normal1 * ln1_gain + ln1_bias).astype(jnp.bfloat16)
    bias_three = jnp.concatenate(
        [bias_qv[:width], jnp.zeros((width,), jnp.float32), bias_qv[width:]]
    )
    query_key_value = (
        jnp.einsum("rsd,de->rse", normed1, w_qkv, preferred_element_type=jnp.float32) + bias_three
    ).astype(jnp.bfloat16)
    query_rows = query_key_value[..., :width]
    key_own = query_key_value[..., width : 2 * width]
    value_own = query_key_value[..., 2 * width :]
    reach = (IMAGE_TOKENS - 2 + span) // span
    offsets = list(range(-reach, reach + 1))
    key_parts = []
    value_parts = []
    for offset in offsets:
        if offset == 0:
            fetched_key, fetched_value = (key_own, value_own)
        else:
            fetched_key, fetched_value = passed_along((key_own, value_own), "seq", -offset)
        key_parts.append(fetched_key)
        value_parts.append(fetched_value)
    key_rows = jnp.concatenate(key_parts, axis=1)
    value_rows = jnp.concatenate(value_parts, axis=1)
    raw_pos = jnp.concatenate(
        [start + offset * span + jnp.arange(span, dtype=jnp.int32) for offset in offsets]
    )
    in_row = (raw_pos >= 0) & (raw_pos < length)
    taken = jnp.take(image_id, jnp.clip(raw_pos, 0, length - 1), axis=1)
    key_ids = jnp.where(in_row[None, :], taken, -1)
    key_pos = jnp.where(in_row, raw_pos, -1)
    key_count = key_rows.shape[1]
    group = block_rows(rows, span)

    def grouped(array):
        return array.reshape((rows // group, group) + array.shape[1:])

    query_heads = grouped(query_rows.reshape(rows, span, ATTENTION_HEADS, HEAD_FEATURES))
    key_heads = grouped(key_rows.reshape(rows, key_count, ATTENTION_HEADS, HEAD_FEATURES))
    value_heads = grouped(value_rows.reshape(rows, key_count, ATTENTION_HEADS, HEAD_FEATURES))
    query_ids = grouped(own_ids)
    grouped_key_ids = grouped(key_ids)

    def forward_block(inputs):
        query_blk, key_blk, value_blk, qid_blk, kid_blk = inputs
        scores = masked_scores(query_blk, key_blk, qid_blk, kid_blk, own_pos, key_pos)
        row_top = jnp.max(scores, axis=-1, keepdims=True)
        total = jnp.sum(jnp.exp(scores - row_top), axis=-1, keepdims=True)
        log_total = row_top + jnp.log(total)
        attention_weights = jnp.exp(scores - log_total).astype(jnp.bfloat16)
        attention_output = jnp.einsum(
            "vbta,vabj->vtbj", attention_weights, value_blk, preferred_element_type=jnp.float32
        )
        return (attention_output.astype(jnp.bfloat16), log_total[..., 0])

    attention_output, log_totals = lax.map(
        forward_block, (query_heads, key_heads, value_heads, query_ids, grouped_key_ids)
    )
    attention_output = attention_output.reshape(rows, span, width)
    hidden1 = (
        inserted
        + jnp.einsum("rsd,de->rse", attention_output, w_out, preferred_element_type=jnp.float32)
        + bias_out
    )
    normal2, inverse2 = normalize(hidden1)
    normed2 = (normal2 * ln2_gain + ln2_bias).astype(jnp.bfloat16)
    upper = jnp.einsum("rsd,df->rsf", normed2, w_up, preferred_element_type=jnp.float32) + bias_up
    activated, gelu_pull = jax.vjp(lambda inner: jax.nn.gelu(inner, approximate=False), upper)
    activated = activated.astype(jnp.bfloat16)
    output = (
        hidden1
        + jnp.einsum("rsf,fd->rsd", activated, w_down, preferred_element_type=jnp.float32)
        + bias_down
    ).astype(jnp.bfloat16)
    out_grad = cotangent.astype(jnp.float32) * valid[..., None]
    act_grad = jnp.einsum(
        "rsd,fd->rsf", out_grad.astype(jnp.bfloat16), w_down, preferred_element_type=jnp.float32
    )
    upper_grad = gelu_pull(act_grad)[0].astype(jnp.bfloat16)
    normed2_grad = jnp.einsum("rsf,df->rsd", upper_grad, w_up, preferred_element_type=jnp.float32)
    hidden1_grad = out_grad + norm_back(normed2_grad, normal2, inverse2, ln2_gain)
    attended_grad = jnp.einsum(
        "rse,de->rsd", hidden1_grad.astype(jnp.bfloat16), w_out, preferred_element_type=jnp.float32
    ).astype(jnp.bfloat16)
    attended_grad = grouped(attended_grad.reshape(rows, span, ATTENTION_HEADS, HEAD_FEATURES))

    def backward_block(inputs):
        query_blk, key_blk, value_blk, qid_blk, kid_blk, total_blk, grad_blk = inputs
        scores = masked_scores(query_blk, key_blk, qid_blk, kid_blk, own_pos, key_pos)
        attention_weights = jnp.exp(scores - total_blk[..., None])
        value_grad = jnp.einsum(
            "ghqk,gqhd->gkhd",
            attention_weights.astype(jnp.bfloat16),
            grad_blk,
            preferred_element_type=jnp.float32,
        )
        prob_grad = jnp.einsum(
            "gqhd,gkhd->ghqk", grad_blk, value_blk, preferred_element_type=jnp.float32
        )
        inner = jnp.sum(attention_weights * prob_grad, axis=-1, keepdims=True)
        score_grad = (attention_weights * (prob_grad - inner)).astype(jnp.bfloat16)
        query_grad = jnp.einsum(
            "vbta,vabj->vtbj", score_grad, key_blk, preferred_element_type=jnp.float32
        ) * HEAD_FEATURES ** (-0.5)
        key_grad = jnp.einsum(
            "ghqk,gqhd->gkhd", score_grad, query_blk, preferred_element_type=jnp.float32
        ) * HEAD_FEATURES ** (-0.5)
        return (query_grad, key_grad, value_grad)

    query_grad, key_grad, value_grad = lax.map(
        backward_block,
        (
            query_heads,
            key_heads,
            value_heads,
            query_ids,
            grouped_key_ids,
            log_totals,
            attended_grad,
        ),
    )
    query_grad = query_grad.reshape(rows, span, width)
    key_grad = key_grad.reshape(rows, key_count, width)
    value_grad = value_grad.reshape(rows, key_count, width)
    key_total = key_grad[:, reach * span : (reach + 1) * span]
    value_total = value_grad[:, reach * span : (reach + 1) * span]
    for offset in range(-reach, reach + 1):
        if offset != 0:
            first = (offset + reach) * span
            back_key, back_value = (
                passed_along(
                    key_grad[:, first : first + span].astype(jnp.bfloat16), "seq", offset
                ).astype(jnp.float32),
                passed_along(
                    value_grad[:, first : first + span].astype(jnp.bfloat16), "seq", offset
                ).astype(jnp.float32),
            )
            key_total = key_total + back_key
            value_total = value_total + back_value
    qkv_grad = jnp.concatenate([query_grad, key_total, value_total], axis=-1).astype(jnp.bfloat16)
    normed1_grad = jnp.einsum("rse,de->rsd", qkv_grad, w_qkv, preferred_element_type=jnp.float32)
    inserted_grad = hidden1_grad + norm_back(normed1_grad, normal1, inverse1, ln1_gain)
    token_gradient = jnp.where(is_prompt, 0.0, inserted_grad).astype(jnp.bfloat16)
    prompt_part = jnp.einsum("rsn,rsd->nd", one_hot, inserted_grad, precision=lax.Precision.HIGHEST)
    prompt_gradient = lax.psum(prompt_part, ("batch", "seq"))
    return (output, token_gradient, prompt_gradient)


def solution(mesh):
    in_specs = (
        P("batch", "seq", None),
        P(),
        P("batch", None),
        P("batch", "seq"),
        P(),
        P(),
        P(),
        P(),
        P(),
        P(),
        P(),
        P(),
        P(),
        P(),
        P(),
        P(),
        P("batch", "seq", None),
    )
    out_specs = (P("batch", "seq", None), P("batch", "seq", None), P())
    return jax.shard_map(body, mesh=mesh, in_specs=in_specs, out_specs=out_specs, check_vma=False)
```

profile of v0, /device:TPU:8, one launch (start us, length us, event | category | flops | bytes accessed | tf_op | source)
XLA Modules:
  0.0 715.2 jit_solution(10487192284243288981)
XLA Ops:
  45.8 81.3 %collective-permute-done.3 = bf16[4,256,768]{2,1,0:T(8,128)(2,1)} collective-permute-done((bf16[4,256,768]{2,1,0:T(8,128)(2,1)}, bf16[4,256,768]{2,1,0:T(8,128)(2,1)}, u32[]{:S(2)}, u32[]{:S(2)}) %collective-permute-start.3) | collective-permute-done | bytes 1572896 | tf_op jit(solution)/shard_map/ppermute | solution.py:16
  131.0 6.6 copy.37
  137.6 22.0 %collective-permute-done.1 = bf16[4,256,768]{2,1,0:T(8,128)(2,1)} collective-permute-done((bf16[4,256,768]{2,1,0:T(8,128)(2,1)}, bf16[4,256,768]{2,1,0:T(8,128)(2,1)}, u32[]{:S(2)}, u32[]{:S(2)}) %collective-permute-start.1) | collective-permute-done | bytes 1572896 | tf_op jit(solution)/shard_map/ppermute | solution.py:16
  163.6 6.6 copy.33
  170.2 47.5 %while.28 = (s32[]{:T(128)}, bf16[2,2,256,12,64]{2,4,3,1,0:T(8,128)(2,1)}, f32[2,2,12,256]{3,2,1,0:T(8,128)}, bf16[2,2,768,12,64]{2,4,3,1,0:T(8,128)(2,1)}, s32[...) while((s32[]{:T(128)}, ...), condition=%wide.region_5.6_spmd.clone, body=%wide.region_2.5_spmd.clone.sunk | while | flops 1261628160 | bytes 141033712 | solution.py:137
  171.4 5.4 fusion.151
  176.8 4.6 exponential_reduce_fusion.2
  183.3 10.4 %fusion.152 = bf16[2,2,256,12,64]{2,4,3,1,0:T(8,128)(2,1)} fusion(bf16[2,2,256,12,64]{2,4,3,1,0:T(8,128)(2,1)} %get-tuple-element.464, s32[]{:T(128)S(6)} %copy.54, f32[2,12,256,768]{3,2,1,0:T(8,128)} %copy-done.2, f32[2,12,256]{2,1,0:T(8,128)S(1)} %get-tuple-element.433, pred[2,256,768]{2,1,0:T(8,128)(4,1)S(1)} %and_or_fusion.4, ...), kind=kOutput, calls=%fused_computation.17.clone.1 | convolution fusion | flops 623247360 | bytes 22438912 | tf_op jit(solution)/shard_map/while/body/eval_jaxpr/vbta,vabj->vtbj/dot_general | solution.py:132
  195.0 5.4 fusion.151
  200.4 4.6 exponential_reduce_fusion.2
  206.9 10.4 %fusion.152 = bf16[2,2,256,12,64]{2,4,3,1,0:T(8,128)(2,1)} fusion(bf16[2,2,256,12,64]{2,4,3,1,0:T(8,128)(2,1)} %get-tuple-element.464, s32[]{:T(128)S(6)} %copy.54, f32[2,12,256,768]{3,2,1,0:T(8,128)} %copy-done.2, f32[2,12,256]{2,1,0:T(8,128)S(1)} %get-tuple-element.433, pred[2,256,768]{2,1,0:T(8,128)(4,1)S(1)} %and_or_fusion.4, ...), kind=kOutput, calls=%fused_computation.17.clone.1 | convolution fusion | flops 623247360 | bytes 22438912 | tf_op jit(solution)/shard_map/while/body/eval_jaxpr/vbta,vabj->vtbj/dot_general | solution.py:132
  222.8 11.3 %fusion.95 = (u8[256,3072]{1,0:T(8,128)(4,1)S(1)}, u8[256,3072]{1,0:T(8,128)(4,1)S(1)}, f32[4,256,3072]{2,1,0:T(8,128)S(1)}) fusion(f32[3072]{0:T(1024)S(1)} %copy-done.29, bf16[768,3072]{1,0:T(8,128)(2,1)} %param.33, f32[4,256,768]{2,1,0:T(8,128)S(1)} %get-tuple-element.285, f32[768]{0:T(1024)S(1)} %copy-done.39, f32[768]{0:T(1024)S(1)} %copy-done.36, ...), kind=kOutput, calls=%fused_computation.138 | convolution fusion | flops 4878237696 | bytes 22046720 | tf_op jit(solution)/shard_map/rsd,df->rsf/dot_general | solution.py:148
  234.1 28.7 %fusion.63 = f32[4,256,3072]{2,1,0:T(8,128)} fusion(f32[4,256,3072]{2,1,0:T(8,128)S(1)} %get-tuple-element.286, f32[3072]{0:T(1024)S(1)} %copy-done.29, u8[256,3072]{1,0:T(8,128)(4,1)S(1)} %get-tuple-element.206, u8[256,3072]{1,0:T(8,128)(4,1)S(1)} %get-tuple-element.205), kind=kLoop, calls=%fused_computation.76 | loop fusion | flops 213909504 | bytes 26750976 | tf_op jit(solution)/shard_map/jvp()/erfc | solution.py:149
  262.8 20.7 %multiply_reduce_fusion.6 = (f32[4,256]{1,0:T(4,128)}, f32[4,256]{1,0:T(4,128)}, f32[4,256,768]{2,1,0:T(8,128)}) fusion(f32[768]{0:T(1024)} %param.31, f32[4,256]{1,0:T(4,128)} %copy-done.21, f32[4,256,768]{2,1,0:T(8,128)} %copy-done.6, f32[4,256]{1,0:T(4,128)} %copy-done.16, bf16[768,3072]{1,0:T(8,128)(2,1)} %param.33, f32[4,256,3072]{2,1,0:T(8,128)} %fusion.63, ...), kind=kOutput, calls=%fused_computation.142 | convolution fusion | flops 9717938176 | bytes 42503168 | tf_op jit(solution)/shard_map/rsf,df->rsd/dot_general | solution.py:161
  285.5 7.0 convolution_convert_fusion
  295.0 114.5 %while.29 = (s32[]{:T(128)}, bf16[2,2,256,12,64]{2,4,3,1,0:T(8,128)(2,1)}, f32[2,2,768,12,64]{2,4,3,1,0:T(8,128)}, f32[2,2,768,12,64]{2,4,3,1,0:T(8,128)}, bf16[...) while((s32[]{:T(128)}, ...), condition=%wide.region_12.13_spmd.clone, body=%wide.region_10.12_spmd.clone.sunk | while | flops 3093621504 | bytes 260910336 | solution.py:191
  297.2 4.6 fusion.161
  301.8 6.4 copy-done.1
  308.2 7.7 %bitcast_dynamic-update-slice_fusion.11 = f32[2,2,768,12,64]{2,4,3,1,0:T(8,128)} fusion(f32[2,2,768,12,64]{2,4,3,1,0:T(8,128)} %get-tuple-element.502, s32[]{:T(128)S(6)} %copy.64, f32[2,12,256,768]{3,2,1,0:T(8,128)S(1)} %fusion.161, f32[2,12,256]{2,1,0:T(8,128)S(1)} %dynamic-slice_bitcast_fusion.9, pred[2,256,768]{2,1,0:T(8,128)(4,1)S(1)} %and_or_fusion.5, ...), kind=kOutput, calls=%fused_computation.40.clone.1 | convolution fusion | flops 622854144 | bytes 24798208 | tf_op jit(solution)/shard_map/while/body/eval_jaxpr/ghqk,gqhd->gkhd/dot_general | solution.py:172
  315.9 15.0 %multiply_reduce_fusion.8 = (f32[2,12,256]{2,1,0:T(8,128)S(1)}, f32[2,12,256,768]{3,2,1,0:T(8,128)}) fusion(f32[2,12,256,768]{3,2,1,0:T(8,128)} %copy-done.1, f32[2,12,256]{2,1,0:T(8,128)S(1)} %dynamic-slice_bitcast_fusion.9, pred[2,256,768]{2,1,0:T(8,128)(4,1)S(1)} %and_or_fusion.5, bf16[2,2,768,12,64]{2,4,3,1,0:T(8,128)(2,1)} %get-tuple-element.524, ...), kind=kOutput, calls=%fused_computation.32.clone.1 | convolution fusion | flops 627566592 | bytes 41337856 | tf_op jit(solution)/shard_map/while/body/eval_jaxpr/gqhd,gkhd->ghqk/dot_general | solution.py:178
  330.9 13.5 %multiply_convert_fusion.6 = bf16[2,12,256,768]{3,2,1,0:T(8,128)(2,1)S(1)} fusion(f32[2,12,256,768]{3,2,1,0:T(8,128)} %get-tuple-element.450, f32[2,12,256,768]{3,2,1,0:T(8,128)} %copy-done.1, f32[2,12,256]{2,1,0:T(8,128)S(1)} %get-tuple-element.451, f32[2,12,256]{2,1,0:T(8,128)S(1)} %dynamic-slice_bitcast_fusion.9, ...), kind=kLoop, calls=%fused_computation.31.clone.1 | loop fusion | flops 28311552 | bytes 47628288 | tf_op jit(solution)/shard_map/while/body/eval_jaxpr/convert_element_type | solution.py:182
  358.8 6.4 copy-done.1
  365.3 7.7 %bitcast_dynamic-update-slice_fusion.11 = f32[2,2,768,12,64]{2,4,3,1,0:T(8,128)} fusion(f32[2,2,768,12,64]{2,4,3,1,0:T(8,128)} %get-tuple-element.502, s32[]{:T(128)S(6)} %copy.64, f32[2,12,256,768]{3,2,1,0:T(8,128)S(1)} %fusion.161, f32[2,12,256]{2,1,0:T(8,128)S(1)} %dynamic-slice_bitcast_fusion.9, pred[2,256,768]{2,1,0:T(8,128)(4,1)S(1)} %and_or_fusion.5, ...), kind=kOutput, calls=%fused_computation.40.clone.1 | convolution fusion | flops 622854144 | bytes 24798208 | tf_op jit(solution)/shard_map/while/body/eval_jaxpr/ghqk,gqhd->gkhd/dot_general | solution.py:172
  372.9 15.0 %multiply_reduce_fusion.8 = (f32[2,12,256]{2,1,0:T(8,128)S(1)}, f32[2,12,256,768]{3,2,1,0:T(8,128)}) fusion(f32[2,12,256,768]{3,2,1,0:T(8,128)} %copy-done.1, f32[2,12,256]{2,1,0:T(8,128)S(1)} %dynamic-slice_bitcast_fusion.9, pred[2,256,768]{2,1,0:T(8,128)(4,1)S(1)} %and_or_fusion.5, bf16[2,2,768,12,64]{2,4,3,1,0:T(8,128)(2,1)} %get-tuple-element.524, ...), kind=kOutput, calls=%fused_computation.32.clone.1 | convolution fusion | flops 627566592 | bytes 41337856 | tf_op jit(solution)/shard_map/while/body/eval_jaxpr/gqhd,gkhd->ghqk/dot_general | solution.py:178
  388.0 13.5 %multiply_convert_fusion.6 = bf16[2,12,256,768]{3,2,1,0:T(8,128)(2,1)S(1)} fusion(f32[2,12,256,768]{3,2,1,0:T(8,128)} %get-tuple-element.450, f32[2,12,256,768]{3,2,1,0:T(8,128)} %copy-done.1, f32[2,12,256]{2,1,0:T(8,128)S(1)} %get-tuple-element.451, f32[2,12,256]{2,1,0:T(8,128)S(1)} %dynamic-slice_bitcast_fusion.9, ...), kind=kLoop, calls=%fused_computation.31.clone.1 | loop fusion | flops 28311552 | bytes 47628288 | tf_op jit(solution)/shard_map/while/body/eval_jaxpr/convert_element_type | solution.py:182
  409.5 9.6 %copy.42 = f32[4,768,768]{2,1,0:T(8,128)} copy(f32[4,768,768]{1,2,0:T(8,128)} %bitcast.177) | data formatting | bytes 18874368 | tf_op jit(solution)/shard_map/reshape | solution.py:205
  431.4 9.7 %copy.40 = f32[4,768,768]{2,1,0:T(8,128)} copy(f32[4,768,768]{1,2,0:T(8,128)} %bitcast.178) | data formatting | bytes 18874368 | tf_op jit(solution)/shard_map/reshape | solution.py:204
  447.1 4.7 collective-permute-start.4
  456.4 76.0 %collective-permute-done.6 = bf16[4,256,768]{2,1,0:T(8,128)(2,1)} collective-permute-done((bf16[4,256,768]{2,1,0:T(8,128)(2,1)}, bf16[4,256,768]{2,1,0:T(8,128)(2,1)}, u32[]{:S(2)}, u32[]{:S(2)}) %collective-permute-start.6) | collective-permute-done | bytes 1572896 | tf_op jit(solution)/shard_map/ppermute | solution.py:16
  535.8 29.7 %collective-permute-done.4 = bf16[4,256,768]{2,1,0:T(8,128)(2,1)} collective-permute-done((bf16[4,256,768]{2,1,0:T(8,128)(2,1)}, bf16[4,256,768]{2,1,0:T(8,128)(2,1)}, u32[]{:S(2)}, u32[]{:S(2)}) %collective-permute-start.4) | collective-permute-done | bytes 1572896 | tf_op jit(solution)/shard_map/ppermute | solution.py:16
  578.7 14.3 %add_convert_fusion.3 = bf16[4,256,768]{2,1,0:T(8,128)(2,1)} fusion(f32[4,256,768]{2,1,0:T(8,128)} %copy-done.6, bf16[3072,768]{1,0:T(8,128)(2,1)} %param.35, f32[4,256,3072]{2,1,0:T(8,128)} %fusion.63, f32[4,256,3072]{2,1,0:T(8,128)} %copy-done.8, f32[3072]{0:T(1024)S(1)} %copy-done.30, f32[768]{0:T(1024)S(1)} %copy-done.40), kind=kOutput, calls=%fused_computation.130 | convolution fusion | flops 4846780416 | bytes 34618368 | tf_op jit(solution)/shard_map/rsf,fd->rsd/dot_general | solution.py:153
  593.0 113.5 %all-reduce.2.cloned.1.call-done = f32[50,768]{1,0:T(8,128)} async-done(((f32[50,768]{1,0:T(8,128)}), f32[50,768]{1,0:T(8,128)}) %all-reduce.2.cloned.1.call-update) | async-done | bytes 153616 | tf_op jit(solution)/shard_map/psum | solution.py:226
  (192 shorter events, 127.1 us)
Async XLA Ops:
  7.2 6.3 copy-start
  7.2 6.3 copy-start.34
  7.2 699.4 %all-reduce.2.cloned.1.call-start = ((), (), s32[]{:S(2)}) async-start(), calls=%async_computation | async-start | bytes 344064 | tf_op jit(solution)/shard_map/psum | solution.py:226
  20.2 106.9 %collective-permute-start.3 = (bf16[4,256,768]{2,1,0:T(8,128)(2,1)}, bf16[4,256,768]{2,1,0:T(8,128)(2,1)}, u32[]{:S(2)}, u32[]{:S(2)}) collective-permute-start(bf16[4,256,768]{2,1,0:T(8,128)(2,1)} %get-tuple-element.275), channel_id=1, source_target_pairs={{1,0},{2,1},{3,2},{4,3},{5,4},{6,5},{7,6},{9,8},{10,9},{11,10},{12... | collective-permute-start | bytes 4718600 | tf_op jit(solution)/shard_map/ppermute | solution.py:16
  23.5 103.6 %collective-permute-start.2 = (bf16[4,256,768]{2,1,0:T(8,128)(2,1)}, bf16[4,256,768]{2,1,0:T(8,128)(2,1)}, u32[]{:S(2)}, u32[]{:S(2)}) collective-permute-start(bf16[4,256,768]{2,1,0:T(8,128)(2,1)} %get-tuple-element.275), channel_id=1, source_target_pairs={{0,1},{1,2},{2,3},{3,4},{4,5},{5,6},{6,7},{8,9},{9,10},{10,11},{11... | collective-permute-start | bytes 4718600 | tf_op jit(solution)/shard_map/ppermute | solution.py:16
  26.0 133.6 %collective-permute-start.1 = (bf16[4,256,768]{2,1,0:T(8,128)(2,1)}, bf16[4,256,768]{2,1,0:T(8,128)(2,1)}, u32[]{:S(2)}, u32[]{:S(2)}) collective-permute-start(bf16[4,256,768]{2,1,0:T(8,128)(2,1)} %get-tuple-element.277), channel_id=1, source_target_pairs={{1,0},{2,1},{3,2},{4,3},{5,4},{6,5},{7,6},{9,8},{10,9},{11,10},{12... | collective-permute-start | bytes 4718600 | tf_op jit(solution)/shard_map/ppermute | solution.py:16
  30.3 129.4 %collective-permute-start = (bf16[4,256,768]{2,1,0:T(8,128)(2,1)}, bf16[4,256,768]{2,1,0:T(8,128)(2,1)}, u32[]{:S(2)}, u32[]{:S(2)}) collective-permute-start(bf16[4,256,768]{2,1,0:T(8,128)(2,1)} %get-tuple-element.277), channel_id=1, source_target_pairs={{0,1},{1,2},{2,3},{3,4},{4,5},{5,6},{6,7},{8,9},{9,10},{10,11},{11... | collective-permute-start | bytes 4718600 | tf_op jit(solution)/shard_map/ppermute | solution.py:16
  176.8 6.4 copy-start.2
  176.8 6.4 copy-start.12
  183.3 10.4 %copy-start.13 = (f32[2,2,12,256]{3,2,1,0:T(8,128)}, f32[2,2,12,256]{3,2,1,0:T(8,128)S(1)}, u32[]{:S(2)}) copy-start(f32[2,2,12,256]{3,2,1,0:T(8,128)S(1)} %get-tuple-element.476) | copy-start | bytes 147460 | tf_op jit(solution)/shard_map/while
  200.4 6.4 copy-start.2
  200.4 6.4 copy-start.12
  206.9 10.4 %copy-start.13 = (f32[2,2,12,256]{3,2,1,0:T(8,128)}, f32[2,2,12,256]{3,2,1,0:T(8,128)S(1)}, u32[]{:S(2)}) copy-start(f32[2,2,12,256]{3,2,1,0:T(8,128)S(1)} %get-tuple-element.476) | copy-start | bytes 147460 | tf_op jit(solution)/shard_map/while
  222.2 11.9 %copy-start.6 = (f32[4,256,768]{2,1,0:T(8,128)}, f32[4,256,768]{2,1,0:T(8,128)S(1)}, u32[]{:S(2)}) copy-start(f32[4,256,768]{2,1,0:T(8,128)S(1)} %get-tuple-element.285) | copy-start | bytes 9437188
  222.2 11.9 %copy-start.16 = (f32[4,256]{1,0:T(4,128)}, f32[4,256]{1,0:T(4,128)S(1)}, u32[]{:S(2)}) copy-start(f32[4,256]{1,0:T(4,128)S(1)} %broadcast_multiply_fusion.4) | copy-start | bytes 12292
  222.7 11.4 %copy-start.21 = (f32[4,256]{1,0:T(4,128)}, f32[4,256]{1,0:T(4,128)S(1)}, u32[]{:S(2)}) copy-start(f32[4,256]{1,0:T(4,128)S(1)} %add_rsqrt_fusion) | copy-start | bytes 12292
  234.1 28.7 %copy-start.8 = (f32[4,256,3072]{2,1,0:T(8,128)}, f32[4,256,3072]{2,1,0:T(8,128)S(1)}, u32[]{:S(2)}) copy-start(f32[4,256,3072]{2,1,0:T(8,128)S(1)} %get-tuple-element.286) | copy-start | bytes 37748740
  301.7 6.4 copy-start.1
  315.9 28.5 %slice-start = ((s8[4718592]{0:T(1024)(128)(4,1)}), s8[524288]{0:T(1024)(128)(4,1)S(1)}, s32[]{:S(2)}) async-start(s8[4718592]{0:T(1024)(128)(4,1)} %bitcast.172), calls=%async_computation.1 | async-start | bytes 1048576 | tf_op jit(solution)/shard_map/while
  330.9 13.5 %slice-start.1 = ((s8[4718592]{0:T(1024)(128)(4,1)}), s8[4194304]{0:T(1024)(128)(4,1)S(1)}, s32[]{:S(2)}) async-start(s8[4718592]{0:T(1024)(128)(4,1)} %bitcast.172), calls=%async_computation.2 | async-start | bytes 8388608 | tf_op jit(solution)/shard_map/while
  358.8 6.4 copy-start.1
  372.9 28.5 %slice-start = ((s8[4718592]{0:T(1024)(128)(4,1)}), s8[524288]{0:T(1024)(128)(4,1)S(1)}, s32[]{:S(2)}) async-start(s8[4718592]{0:T(1024)(128)(4,1)} %bitcast.172), calls=%async_computation.1 | async-start | bytes 1048576 | tf_op jit(solution)/shard_map/while
  388.0 13.5 %slice-start.1 = ((s8[4718592]{0:T(1024)(128)(4,1)}), s8[4194304]{0:T(1024)(128)(4,1)S(1)}, s32[]{:S(2)}) async-start(s8[4718592]{0:T(1024)(128)(4,1)} %bitcast.172), calls=%async_computation.2 | async-start | bytes 8388608 | tf_op jit(solution)/shard_map/while
  425.1 107.3 %collective-permute-start.6 = (bf16[4,256,768]{2,1,0:T(8,128)(2,1)}, bf16[4,256,768]{2,1,0:T(8,128)(2,1)}, u32[]{:S(2)}, u32[]{:S(2)}) collective-permute-start(bf16[4,256,768]{2,1,0:T(8,128)(2,1)} %get-tuple-element.273), channel_id=1, source_target_pairs={{1,0},{2,1},{3,2},{4,3},{5,4},{6,5},{7,6},{9,8},{10,9},{11,10},{12... | collective-permute-start | bytes 4718600 | tf_op jit(solution)/shard_map/ppermute | solution.py:16
  429.3 103.1 %collective-permute-start.7 = (bf16[4,256,768]{2,1,0:T(8,128)(2,1)}, bf16[4,256,768]{2,1,0:T(8,128)(2,1)}, u32[]{:S(2)}, u32[]{:S(2)}) collective-permute-start(bf16[4,256,768]{2,1,0:T(8,128)(2,1)} %get-tuple-element.274), channel_id=1, source_target_pairs={{0,1},{1,2},{2,3},{3,4},{4,5},{5,6},{6,7},{8,9},{9,10},{10,11},{11... | collective-permute-start | bytes 4718600 | tf_op jit(solution)/shard_map/ppermute | solution.py:16
  447.1 118.4 %collective-permute-start.4 = (bf16[4,256,768]{2,1,0:T(8,128)(2,1)}, bf16[4,256,768]{2,1,0:T(8,128)(2,1)}, u32[]{:S(2)}, u32[]{:S(2)}) collective-permute-start(bf16[4,256,768]{2,1,0:T(8,128)(2,1)} %get-tuple-element.271), channel_id=1, source_target_pairs={{1,0},{2,1},{3,2},{4,3},{5,4},{6,5},{7,6},{9,8},{10,9},{11,10},{12... | collective-permute-start | bytes 4718600 | tf_op jit(solution)/shard_map/ppermute | solution.py:16
  451.8 113.8 %collective-permute-start.5 = (bf16[4,256,768]{2,1,0:T(8,128)(2,1)}, bf16[4,256,768]{2,1,0:T(8,128)(2,1)}, u32[]{:S(2)}, u32[]{:S(2)}) collective-permute-start(bf16[4,256,768]{2,1,0:T(8,128)(2,1)} %get-tuple-element.272), channel_id=1, source_target_pairs={{0,1},{1,2},{2,3},{3,4},{4,5},{5,6},{6,7},{8,9},{9,10},{10,11},{11... | collective-permute-start | bytes 4718600 | tf_op jit(solution)/shard_map/ppermute | solution.py:16
  535.7 33.2 %copy-start.5 = (f32[4,256,768]{2,1,0:T(8,128)S(1)}, f32[4,256,768]{2,1,0:T(8,128)}, u32[]{:S(2)}) copy-start(f32[4,256,768]{2,1,0:T(8,128)} %copy-done.4) | copy-start | bytes 9437188
  535.8 33.2 %copy-start.11 = (bf16[4,256,768]{2,1,0:T(8,128)(2,1)S(1)}, bf16[4,256,768]{2,1,0:T(8,128)(2,1)}, u32[]{:S(2)}) copy-start(bf16[4,256,768]{2,1,0:T(8,128)(2,1)} %copy.44) | copy-start | bytes 4718596
  535.8 33.2 %copy-start.15 = (f32[4,256]{1,0:T(4,128)S(1)}, f32[4,256]{1,0:T(4,128)}, u32[]{:S(2)}) copy-start(f32[4,256]{1,0:T(4,128)} %copy-done.14) | copy-start | bytes 12292
  535.8 33.2 %copy-start.20 = (f32[4,256]{1,0:T(4,128)S(1)}, f32[4,256]{1,0:T(4,128)}, u32[]{:S(2)}) copy-start(f32[4,256]{1,0:T(4,128)} %copy-done.19) | copy-start | bytes 12292
  535.8 33.2 %copy-start.35 = (f32[768]{0:T(1024)S(1)}, f32[768]{0:T(1024)}, u32[]{:S(2)}) copy-start(f32[768]{0:T(1024)} %param.25) | copy-start | bytes 9220
  (27 other events, 108.7 us)
Sparse Core Ops, SparseCore 0:
  578.8 127.6 all-reduce.1
where the time goes:
time: 721 us; the launch traced here: 715 us
  waiting for transfers between devices  323 us (45%)
  matrix products  173 us (24%)
  other arithmetic  102 us (14%)
  local copies, waits for them, and re-layouts  76.2 us (11%)
  starting transfers between devices  25.3 us (4%)
  between operations  14.9 us (2%)
    ppermute x8, waiting for transfers between devices, passed_along(): return lax.ppermute(block, axis, route)  209 us
    psum x1, waiting for transfers between devices, body(): prompt_gradient = lax.psum(prompt_part, ('batch', 'seq'))  114 us
    dot_general x2, matrix products, backward_block(): jnp.einsum('gqhd,gkhd->ghqk', grad_blk, value_blk, preferred_element_type...  30 us
    another operation x1, other arithmetic, body(): jax.nn.gelu(inner, approximate=False)  28.7 us
    convert_element_type x2, other arithmetic, backward_block(): score_grad = (attention_weights * (prob_grad - inner)).astype(jnp.bfloat16)  27 us
    ppermute x8, starting transfers between devices, passed_along(): return lax.ppermute(block, axis, route)  25.2 us
    dot_general x2, matrix products, forward_block(): jnp.einsum('vbta,vabj->vtbj', attention_weights, value_blk, preferred_ele...  20.8 us
    dot_general x1, matrix products, body(): jnp.einsum('rsf,df->rsd', upper_grad, w_up, preferred_element_type=jnp.fl...  20.7 us
  transfers between devices with their start and end apart: 9, of which 6 were waited for; matrix products, arithmetic and copies ran while one was open for 8% of the time, Pallas kernels for 0%

commit v1 on v0

--- a/solution.py
+++ b/solution.py
@@ -223,7 +223,7 @@
     inserted_grad = hidden1_grad + norm_back(normed1_grad, normal1, inverse1, ln1_gain)
     token_gradient = jnp.where(is_prompt, 0.0, inserted_grad).astype(jnp.bfloat16)
     prompt_part = jnp.einsum("rsn,rsd->nd", one_hot, inserted_grad, precision=lax.Precision.HIGHEST)
-    prompt_gradient = lax.psum(prompt_part, ("batch", "seq"))
+    prompt_gradient = jnp.sum(lax.all_gather(prompt_part, ("batch", "seq")), axis=0)
     return (output, token_gradient, prompt_gradient)
 
 

time: 721 us -> 664 us (0.921)
  waiting for transfers between devices: 323 us -> 262 us
    psum x1 -> x0, waiting for transfers between devices: 114 us -> none  [body(): prompt_gradient = lax.psum(prompt_part, ('batch', 'seq'))]
    all_gather x0 -> x1, waiting for transfers between devices: none -> 53.4 us  [body(): lax.all_gather(prompt_part, ('batch', 'seq'))]
  transfers between devices with their start and end apart: 9 -> 9, of which waited for: 6 -> 6; matrix products, arithmetic and copies ran while one was open for 8% -> 9% of each run, Pallas kernels for 0% -> 0%
where the time goes in v1:
time: 664 us; the launch traced here: 657 us
  waiting for transfers between devices  262 us (39%)
  matrix products  173 us (26%)
  other arithmetic  105 us (16%)
  local copies, waits for them, and re-layouts  74.6 us (11%)
  starting transfers between devices  25.3 us (4%)
  between operations  14.9 us (2%)
    ppermute x8, waiting for transfers between devices, passed_along(): return lax.ppermute(block, axis, route)  209 us
    all_gather x1, waiting for transfers between devices, body(): lax.all_gather(prompt_part, ('batch', 'seq'))  53.4 us
    dot_general x2, matrix products, backward_block(): jnp.einsum('gqhd,gkhd->ghqk', grad_blk, value_blk, preferred_element_type...  30 us
    another operation x1, other arithmetic, body(): jax.nn.gelu(inner, approximate=False)  28.7 us
    convert_element_type x2, other arithmetic, backward_block(): score_grad = (attention_weights * (prob_grad - inner)).astype(jnp.bfloat16)  27 us
    ppermute x8, starting transfers between devices, passed_along(): return lax.ppermute(block, axis, route)  25.2 us
    dot_general x2, matrix products, forward_block(): jnp.einsum('vbta,vabj->vtbj', attention_weights, value_blk, preferred_ele...  20.8 us
    dot_general x1, matrix products, body(): jnp.einsum('rsf,df->rsd', upper_grad, w_up, preferred_element_type=jnp.fl...  20.7 us
  transfers between devices with their start and end apart: 9, of which 6 were waited for; matrix products, arithmetic and copies ran while one was open for 9% of the time, Pallas kernels for 0%

profile of v1, /device:TPU:8, one launch (start us, length us, event | category | flops | bytes accessed | tf_op | source)
XLA Modules:
  0.0 657.0 jit_solution(6317752355086786806)
XLA Ops:
  45.8 81.3 %collective-permute-done.3 = bf16[4,256,768]{2,1,0:T(8,128)(2,1)} collective-permute-done((bf16[4,256,768]{2,1,0:T(8,128)(2,1)}, bf16[4,256,768]{2,1,0:T(8,128)(2,1)}, u32[]{:S(2)}, u32[]{:S(2)}) %collective-permute-start.3) | collective-permute-done | bytes 1572896 | tf_op jit(solution)/shard_map/ppermute | solution.py:16
  131.0 6.6 %copy.49 = bf16[4,768,768]{1,2,0:T(8,128)(2,1)} copy(bf16[4,768,768]{2,1,0:T(8,128)(2,1)} %pad_maximum_fusion.1) | data formatting | bytes 9437184 | tf_op jit(solution)/shard_map/concatenate | solution.py:104
  137.6 22.0 %collective-permute-done.1 = bf16[4,256,768]{2,1,0:T(8,128)(2,1)} collective-permute-done((bf16[4,256,768]{2,1,0:T(8,128)(2,1)}, bf16[4,256,768]{2,1,0:T(8,128)(2,1)}, u32[]{:S(2)}, u32[]{:S(2)}) %collective-permute-start.1) | collective-permute-done | bytes 1572896 | tf_op jit(solution)/shard_map/ppermute | solution.py:16
  163.6 6.6 %copy.45 = bf16[4,768,768]{1,2,0:T(8,128)(2,1)} copy(bf16[4,768,768]{2,1,0:T(8,128)(2,1)} %pad_maximum_fusion) | data formatting | bytes 9437184 | tf_op jit(solution)/shard_map/concatenate | solution.py:105
  170.2 47.5 %while.28 = (s32[]{:T(128)}, bf16[2,2,256,12,64]{2,4,3,1,0:T(8,128)(2,1)}, f32[2,2,12,256]{3,2,1,0:T(8,128)}, bf16[2,2,768,12,64]{2,4,3,1,0:T(8,128)(2,1)}, s32[...) while((s32[]{:T(128)}, ...), condition=%wide.region_5.6_spmd.clone, body=%wide.region_2.5_spmd.clone.sunk | while | flops 1261628160 | bytes 141033712 | solution.py:137
  171.4 5.4 fusion.151
  176.8 4.6 exponential_reduce_fusion.2
  183.3 10.4 %fusion.152 = bf16[2,2,256,12,64]{2,4,3,1,0:T(8,128)(2,1)} fusion(bf16[2,2,256,12,64]{2,4,3,1,0:T(8,128)(2,1)} %get-tuple-element.464, s32[]{:T(128)S(6)} %copy.66, f32[2,12,256,768]{3,2,1,0:T(8,128)} %copy-done.2, f32[2,12,256]{2,1,0:T(8,128)S(1)} %get-tuple-element.433, pred[2,256,768]{2,1,0:T(8,128)(4,1)S(1)} %and_or_fusion.4, ...), kind=kOutput, calls=%fused_computation.17.clone.1 | convolution fusion | flops 623247360 | bytes 22438912 | tf_op jit(solution)/shard_map/while/body/eval_jaxpr/vbta,vabj->vtbj/dot_general | solution.py:132
  195.0 5.4 fusion.151
  200.4 4.6 exponential_reduce_fusion.2
  206.9 10.4 %fusion.152 = bf16[2,2,256,12,64]{2,4,3,1,0:T(8,128)(2,1)} fusion(bf16[2,2,256,12,64]{2,4,3,1,0:T(8,128)(2,1)} %get-tuple-element.464, s32[]{:T(128)S(6)} %copy.66, f32[2,12,256,768]{3,2,1,0:T(8,128)} %copy-done.2, f32[2,12,256]{2,1,0:T(8,128)S(1)} %get-tuple-element.433, pred[2,256,768]{2,1,0:T(8,128)(4,1)S(1)} %and_or_fusion.4, ...), kind=kOutput, calls=%fused_computation.17.clone.1 | convolution fusion | flops 623247360 | bytes 22438912 | tf_op jit(solution)/shard_map/while/body/eval_jaxpr/vbta,vabj->vtbj/dot_general | solution.py:132
  222.8 11.3 %fusion.95 = (u8[256,3072]{1,0:T(8,128)(4,1)S(1)}, u8[256,3072]{1,0:T(8,128)(4,1)S(1)}, f32[4,256,3072]{2,1,0:T(8,128)S(1)}) fusion(f32[3072]{0:T(1024)S(1)} %copy-done.29, bf16[768,3072]{1,0:T(8,128)(2,1)} %param.33, f32[4,256,768]{2,1,0:T(8,128)S(1)} %get-tuple-element.285, f32[768]{0:T(1024)S(1)} %copy-done.39, f32[768]{0:T(1024)S(1)} %copy-done.36, ...), kind=kOutput, calls=%fused_computation.138 | convolution fusion | flops 4878237696 | bytes 22046720 | tf_op jit(solution)/shard_map/rsd,df->rsf/dot_general | solution.py:148
  234.1 28.7 %fusion.63 = f32[4,256,3072]{2,1,0:T(8,128)} fusion(f32[4,256,3072]{2,1,0:T(8,128)S(1)} %get-tuple-element.286, f32[3072]{0:T(1024)S(1)} %copy-done.29, u8[256,3072]{1,0:T(8,128)(4,1)S(1)} %get-tuple-element.206, u8[256,3072]{1,0:T(8,128)(4,1)S(1)} %get-tuple-element.205), kind=kLoop, calls=%fused_computation.76 | loop fusion | flops 213909504 | bytes 26750976 | tf_op jit(solution)/shard_map/jvp()/erfc | solution.py:149
  262.8 20.7 %multiply_reduce_fusion.6 = (f32[4,256]{1,0:T(4,128)}, f32[4,256]{1,0:T(4,128)}, f32[4,256,768]{2,1,0:T(8,128)}) fusion(f32[768]{0:T(1024)} %param.31, f32[4,256]{1,0:T(4,128)} %copy-done.21, f32[4,256,768]{2,1,0:T(8,128)} %copy-done.6, f32[4,256]{1,0:T(4,128)} %copy-done.16, bf16[768,3072]{1,0:T(8,128)(2,1)} %param.33, f32[4,256,3072]{2,1,0:T(8,128)} %fusion.63, ...), kind=kOutput, calls=%fused_computation.142 | convolution fusion | flops 9717938176 | bytes 42503168 | tf_op jit(solution)/shard_map/rsf,df->rsd/dot_general | solution.py:161
  285.4 7.0 %convolution_convert_fusion = bf16[4,256,768]{2,1,0:T(8,128)(2,1)} fusion(bf16[768,768]{1,0:T(8,128)(2,1)} %param.29, bf16[4,256,768]{2,1,0:T(8,128)(2,1)} %param.37, f32[4,256,768]{2,1,0:T(8,128)} %get-tuple-element.287, f32[4,256,768]{2,1,0:T(8,128)} %copy-done.6, f32[4,256]{1,0:T(4,128)S(1)} %broadcast_multiply_fusion.2, ...), kind=kOutput, calls=%fused_computation.143 | convolution fusion | flops 1217396736 | bytes 10640384 | tf_op jit(solution)/shard_map/rse,de->rsd/dot_general | solution.py:163
  295.0 114.5 %while.29 = (s32[]{:T(128)}, bf16[2,2,256,12,64]{2,4,3,1,0:T(8,128)(2,1)}, f32[2,2,768,12,64]{2,4,3,1,0:T(8,128)}, f32[2,2,768,12,64]{2,4,3,1,0:T(8,128)}, bf16[...) while((s32[]{:T(128)}, ...), condition=%wide.region_12.13_spmd.clone, body=%wide.region_10.12_spmd.clone.sunk | while | flops 3093621504 | bytes 260910336 | solution.py:191
  297.2 4.6 fusion.161
  301.7 6.4 copy-done.1
  308.2 7.7 %bitcast_dynamic-update-slice_fusion.11 = f32[2,2,768,12,64]{2,4,3,1,0:T(8,128)} fusion(f32[2,2,768,12,64]{2,4,3,1,0:T(8,128)} %get-tuple-element.502, s32[]{:T(128)S(6)} %copy.76, f32[2,12,256,768]{3,2,1,0:T(8,128)S(1)} %fusion.161, f32[2,12,256]{2,1,0:T(8,128)S(1)} %dynamic-slice_bitcast_fusion.9, pred[2,256,768]{2,1,0:T(8,128)(4,1)S(1)} %and_or_fusion.5, ...), kind=kOutput, calls=%fused_computation.40.clone.1 | convolution fusion | flops 622854144 | bytes 24798208 | tf_op jit(solution)/shard_map/while/body/eval_jaxpr/ghqk,gqhd->gkhd/dot_general | solution.py:172
  315.8 15.0 %multiply_reduce_fusion.8 = (f32[2,12,256]{2,1,0:T(8,128)S(1)}, f32[2,12,256,768]{3,2,1,0:T(8,128)}) fusion(f32[2,12,256,768]{3,2,1,0:T(8,128)} %copy-done.1, f32[2,12,256]{2,1,0:T(8,128)S(1)} %dynamic-slice_bitcast_fusion.9, pred[2,256,768]{2,1,0:T(8,128)(4,1)S(1)} %and_or_fusion.5, bf16[2,2,768,12,64]{2,4,3,1,0:T(8,128)(2,1)} %get-tuple-element.524, ...), kind=kOutput, calls=%fused_computation.32.clone.1 | convolution fusion | flops 627566592 | bytes 41337856 | tf_op jit(solution)/shard_map/while/body/eval_jaxpr/gqhd,gkhd->ghqk/dot_general | solution.py:178
  330.9 13.5 %multiply_convert_fusion.6 = bf16[2,12,256,768]{3,2,1,0:T(8,128)(2,1)S(1)} fusion(f32[2,12,256,768]{3,2,1,0:T(8,128)} %get-tuple-element.450, f32[2,12,256,768]{3,2,1,0:T(8,128)} %copy-done.1, f32[2,12,256]{2,1,0:T(8,128)S(1)} %get-tuple-element.451, f32[2,12,256]{2,1,0:T(8,128)S(1)} %dynamic-slice_bitcast_fusion.9, ...), kind=kLoop, calls=%fused_computation.31.clone.1 | loop fusion | flops 28311552 | bytes 47628288 | tf_op jit(solution)/shard_map/while/body/eval_jaxpr/convert_element_type | solution.py:182
  358.8 6.4 copy-done.1
  365.2 7.7 %bitcast_dynamic-update-slice_fusion.11 = f32[2,2,768,12,64]{2,4,3,1,0:T(8,128)} fusion(f32[2,2,768,12,64]{2,4,3,1,0:T(8,128)} %get-tuple-element.502, s32[]{:T(128)S(6)} %copy.76, f32[2,12,256,768]{3,2,1,0:T(8,128)S(1)} %fusion.161, f32[2,12,256]{2,1,0:T(8,128)S(1)} %dynamic-slice_bitcast_fusion.9, pred[2,256,768]{2,1,0:T(8,128)(4,1)S(1)} %and_or_fusion.5, ...), kind=kOutput, calls=%fused_computation.40.clone.1 | convolution fusion | flops 622854144 | bytes 24798208 | tf_op jit(solution)/shard_map/while/body/eval_jaxpr/ghqk,gqhd->gkhd/dot_general | solution.py:172
  372.9 15.0 %multiply_reduce_fusion.8 = (f32[2,12,256]{2,1,0:T(8,128)S(1)}, f32[2,12,256,768]{3,2,1,0:T(8,128)}) fusion(f32[2,12,256,768]{3,2,1,0:T(8,128)} %copy-done.1, f32[2,12,256]{2,1,0:T(8,128)S(1)} %dynamic-slice_bitcast_fusion.9, pred[2,256,768]{2,1,0:T(8,128)(4,1)S(1)} %and_or_fusion.5, bf16[2,2,768,12,64]{2,4,3,1,0:T(8,128)(2,1)} %get-tuple-element.524, ...), kind=kOutput, calls=%fused_computation.32.clone.1 | convolution fusion | flops 627566592 | bytes 41337856 | tf_op jit(solution)/shard_map/while/body/eval_jaxpr/gqhd,gkhd->ghqk/dot_general | solution.py:178
  387.9 13.5 %multiply_convert_fusion.6 = bf16[2,12,256,768]{3,2,1,0:T(8,128)(2,1)S(1)} fusion(f32[2,12,256,768]{3,2,1,0:T(8,128)} %get-tuple-element.450, f32[2,12,256,768]{3,2,1,0:T(8,128)} %copy-done.1, f32[2,12,256]{2,1,0:T(8,128)S(1)} %get-tuple-element.451, f32[2,12,256]{2,1,0:T(8,128)S(1)} %dynamic-slice_bitcast_fusion.9, ...), kind=kLoop, calls=%fused_computation.31.clone.1 | loop fusion | flops 28311552 | bytes 47628288 | tf_op jit(solution)/shard_map/while/body/eval_jaxpr/convert_element_type | solution.py:182
  409.5 9.6 %copy.54 = f32[4,768,768]{2,1,0:T(8,128)} copy(f32[4,768,768]{1,2,0:T(8,128)} %bitcast.178) | data formatting | bytes 18874368 | tf_op jit(solution)/shard_map/reshape | solution.py:205
  431.4 9.7 %copy.52 = f32[4,768,768]{2,1,0:T(8,128)} copy(f32[4,768,768]{1,2,0:T(8,128)} %bitcast.179) | data formatting | bytes 18874368 | tf_op jit(solution)/shard_map/reshape | solution.py:204
  447.1 4.7 collective-permute-start.4
  456.4 76.0 %collective-permute-done.6 = bf16[4,256,768]{2,1,0:T(8,128)(2,1)} collective-permute-done((bf16[4,256,768]{2,1,0:T(8,128)(2,1)}, bf16[4,256,768]{2,1,0:T(8,128)(2,1)}, u32[]{:S(2)}, u32[]{:S(2)}) %collective-permute-start.6) | collective-permute-done | bytes 1572896 | tf_op jit(solution)/shard_map/ppermute | solution.py:16
  535.8 29.7 %collective-permute-done.4 = bf16[4,256,768]{2,1,0:T(8,128)(2,1)} collective-permute-done((bf16[4,256,768]{2,1,0:T(8,128)(2,1)}, bf16[4,256,768]{2,1,0:T(8,128)(2,1)}, u32[]{:S(2)}, u32[]{:S(2)}) %collective-permute-start.4) | collective-permute-done | bytes 1572896 | tf_op jit(solution)/shard_map/ppermute | solution.py:16
  578.7 14.3 %add_convert_fusion.3 = bf16[4,256,768]{2,1,0:T(8,128)(2,1)} fusion(f32[4,256,768]{2,1,0:T(8,128)} %copy-done.6, bf16[3072,768]{1,0:T(8,128)(2,1)} %param.35, f32[4,256,3072]{2,1,0:T(8,128)} %fusion.63, f32[4,256,3072]{2,1,0:T(8,128)} %copy-done.8, f32[3072]{0:T(1024)S(1)} %copy-done.30, f32[768]{0:T(1024)S(1)} %copy-done.40), kind=kOutput, calls=%fused_computation.130 | convolution fusion | flops 4846780416 | bytes 34618368 | tf_op jit(solution)/shard_map/rsf,fd->rsd/dot_general | solution.py:153
  593.1 53.4 %all-gather.4.cloned.1.call-done = f32[32,50,768]{2,1,0:T(8,128)} async-done(((f32[1,50,768]{2,1,0:T(8,128)}), f32[32,50,768]{2,1,0:T(8,128)}) %all-gather.4.cloned.1.call-update) | async-done | bytes 4915216 | tf_op jit(solution)/shard_map/all_gather | solution.py:226
  (192 shorter events, 129.0 us)
Async XLA Ops:
  7.2 6.3 copy-start
  7.2 6.3 copy-start.34
  7.2 639.3 %all-gather.4.cloned.1.call-start = ((), (), s32[]{:S(2)}) async-start(), calls=%async_computation | async-start | bytes 5677056 | tf_op jit(solution)/shard_map/all_gather | solution.py:226
  20.2 106.9 %collective-permute-start.3 = (bf16[4,256,768]{2,1,0:T(8,128)(2,1)}, bf16[4,256,768]{2,1,0:T(8,128)(2,1)}, u32[]{:S(2)}, u32[]{:S(2)}) collective-permute-start(bf16[4,256,768]{2,1,0:T(8,128)(2,1)} %get-tuple-element.275), channel_id=1, source_target_pairs={{1,0},{2,1},{3,2},{4,3},{5,4},{6,5},{7,6},{9,8},{10,9},{11,10},{12... | collective-permute-start | bytes 4718600 | tf_op jit(solution)/shard_map/ppermute | solution.py:16
  23.5 103.6 %collective-permute-start.2 = (bf16[4,256,768]{2,1,0:T(8,128)(2,1)}, bf16[4,256,768]{2,1,0:T(8,128)(2,1)}, u32[]{:S(2)}, u32[]{:S(2)}) collective-permute-start(bf16[4,256,768]{2,1,0:T(8,128)(2,1)} %get-tuple-element.275), channel_id=1, source_target_pairs={{0,1},{1,2},{2,3},{3,4},{4,5},{5,6},{6,7},{8,9},{9,10},{10,11},{11... | collective-permute-start | bytes 4718600 | tf_op jit(solution)/shard_map/ppermute | solution.py:16
  26.0 133.6 %collective-permute-start.1 = (bf16[4,256,768]{2,1,0:T(8,128)(2,1)}, bf16[4,256,768]{2,1,0:T(8,128)(2,1)}, u32[]{:S(2)}, u32[]{:S(2)}) collective-permute-start(bf16[4,256,768]{2,1,0:T(8,128)(2,1)} %get-tuple-element.277), channel_id=1, source_target_pairs={{1,0},{2,1},{3,2},{4,3},{5,4},{6,5},{7,6},{9,8},{10,9},{11,10},{12... | collective-permute-start | bytes 4718600 | tf_op jit(solution)/shard_map/ppermute | solution.py:16
  30.3 129.4 %collective-permute-start = (bf16[4,256,768]{2,1,0:T(8,128)(2,1)}, bf16[4,256,768]{2,1,0:T(8,128)(2,1)}, u32[]{:S(2)}, u32[]{:S(2)}) collective-permute-start(bf16[4,256,768]{2,1,0:T(8,128)(2,1)} %get-tuple-element.277), channel_id=1, source_target_pairs={{0,1},{1,2},{2,3},{3,4},{4,5},{5,6},{6,7},{8,9},{9,10},{10,11},{11... | collective-permute-start | bytes 4718600 | tf_op jit(solution)/shard_map/ppermute | solution.py:16
  176.8 6.4 copy-start.2
  176.8 6.4 copy-start.12
  183.3 10.4 %copy-start.13 = (f32[2,2,12,256]{3,2,1,0:T(8,128)}, f32[2,2,12,256]{3,2,1,0:T(8,128)S(1)}, u32[]{:S(2)}) copy-start(f32[2,2,12,256]{3,2,1,0:T(8,128)S(1)} %get-tuple-element.476) | copy-start | bytes 147460 | tf_op jit(solution)/shard_map/while
  200.4 6.4 copy-start.2
  200.4 6.4 copy-start.12
  206.9 10.4 %copy-start.13 = (f32[2,2,12,256]{3,2,1,0:T(8,128)}, f32[2,2,12,256]{3,2,1,0:T(8,128)S(1)}, u32[]{:S(2)}) copy-start(f32[2,2,12,256]{3,2,1,0:T(8,128)S(1)} %get-tuple-element.476) | copy-start | bytes 147460 | tf_op jit(solution)/shard_map/while
  222.2 11.9 %copy-start.6 = (f32[4,256,768]{2,1,0:T(8,128)}, f32[4,256,768]{2,1,0:T(8,128)S(1)}, u32[]{:S(2)}) copy-start(f32[4,256,768]{2,1,0:T(8,128)S(1)} %get-tuple-element.285) | copy-start | bytes 9437188
  222.2 11.9 %copy-start.16 = (f32[4,256]{1,0:T(4,128)}, f32[4,256]{1,0:T(4,128)S(1)}, u32[]{:S(2)}) copy-start(f32[4,256]{1,0:T(4,128)S(1)} %broadcast_multiply_fusion.4) | copy-start | bytes 12292
  222.7 11.3 %copy-start.21 = (f32[4,256]{1,0:T(4,128)}, f32[4,256]{1,0:T(4,128)S(1)}, u32[]{:S(2)}) copy-start(f32[4,256]{1,0:T(4,128)S(1)} %add_rsqrt_fusion) | copy-start | bytes 12292
  234.1 28.7 %copy-start.8 = (f32[4,256,3072]{2,1,0:T(8,128)}, f32[4,256,3072]{2,1,0:T(8,128)S(1)}, u32[]{:S(2)}) copy-start(f32[4,256,3072]{2,1,0:T(8,128)S(1)} %get-tuple-element.286) | copy-start | bytes 37748740
  301.7 6.4 copy-start.1
  315.8 28.5 %slice-start = ((s8[4718592]{0:T(1024)(128)(4,1)}), s8[524288]{0:T(1024)(128)(4,1)S(1)}, s32[]{:S(2)}) async-start(s8[4718592]{0:T(1024)(128)(4,1)} %bitcast.173), calls=%async_computation.1 | async-start | bytes 1048576 | tf_op jit(solution)/shard_map/while
  330.9 13.5 %slice-start.1 = ((s8[4718592]{0:T(1024)(128)(4,1)}), s8[4194304]{0:T(1024)(128)(4,1)S(1)}, s32[]{:S(2)}) async-start(s8[4718592]{0:T(1024)(128)(4,1)} %bitcast.173), calls=%async_computation.2 | async-start | bytes 8388608 | tf_op jit(solution)/shard_map/while
  358.8 6.4 copy-start.1
  372.9 28.5 %slice-start = ((s8[4718592]{0:T(1024)(128)(4,1)}), s8[524288]{0:T(1024)(128)(4,1)S(1)}, s32[]{:S(2)}) async-start(s8[4718592]{0:T(1024)(128)(4,1)} %bitcast.173), calls=%async_computation.1 | async-start | bytes 1048576 | tf_op jit(solution)/shard_map/while
  387.9 13.5 %slice-start.1 = ((s8[4718592]{0:T(1024)(128)(4,1)}), s8[4194304]{0:T(1024)(128)(4,1)S(1)}, s32[]{:S(2)}) async-start(s8[4718592]{0:T(1024)(128)(4,1)} %bitcast.173), calls=%async_computation.2 | async-start | bytes 8388608 | tf_op jit(solution)/shard_map/while
  425.1 107.3 %collective-permute-start.6 = (bf16[4,256,768]{2,1,0:T(8,128)(2,1)}, bf16[4,256,768]{2,1,0:T(8,128)(2,1)}, u32[]{:S(2)}, u32[]{:S(2)}) collective-permute-start(bf16[4,256,768]{2,1,0:T(8,128)(2,1)} %get-tuple-element.273), channel_id=1, source_target_pairs={{1,0},{2,1},{3,2},{4,3},{5,4},{6,5},{7,6},{9,8},{10,9},{11,10},{12... | collective-permute-start | bytes 4718600 | tf_op jit(solution)/shard_map/ppermute | solution.py:16
  429.3 103.1 %collective-permute-start.7 = (bf16[4,256,768]{2,1,0:T(8,128)(2,1)}, bf16[4,256,768]{2,1,0:T(8,128)(2,1)}, u32[]{:S(2)}, u32[]{:S(2)}) collective-permute-start(bf16[4,256,768]{2,1,0:T(8,128)(2,1)} %get-tuple-element.274), channel_id=1, source_target_pairs={{0,1},{1,2},{2,3},{3,4},{4,5},{5,6},{6,7},{8,9},{9,10},{10,11},{11... | collective-permute-start | bytes 4718600 | tf_op jit(solution)/shard_map/ppermute | solution.py:16
  447.1 118.4 %collective-permute-start.4 = (bf16[4,256,768]{2,1,0:T(8,128)(2,1)}, bf16[4,256,768]{2,1,0:T(8,128)(2,1)}, u32[]{:S(2)}, u32[]{:S(2)}) collective-permute-start(bf16[4,256,768]{2,1,0:T(8,128)(2,1)} %get-tuple-element.271), channel_id=1, source_target_pairs={{1,0},{2,1},{3,2},{4,3},{5,4},{6,5},{7,6},{9,8},{10,9},{11,10},{12... | collective-permute-start | bytes 4718600 | tf_op jit(solution)/shard_map/ppermute | solution.py:16
  451.8 113.8 %collective-permute-start.5 = (bf16[4,256,768]{2,1,0:T(8,128)(2,1)}, bf16[4,256,768]{2,1,0:T(8,128)(2,1)}, u32[]{:S(2)}, u32[]{:S(2)}) collective-permute-start(bf16[4,256,768]{2,1,0:T(8,128)(2,1)} %get-tuple-element.272), channel_id=1, source_target_pairs={{0,1},{1,2},{2,3},{3,4},{4,5},{5,6},{6,7},{8,9},{9,10},{10,11},{11... | collective-permute-start | bytes 4718600 | tf_op jit(solution)/shard_map/ppermute | solution.py:16
  535.7 33.2 %copy-start.5 = (f32[4,256,768]{2,1,0:T(8,128)S(1)}, f32[4,256,768]{2,1,0:T(8,128)}, u32[]{:S(2)}) copy-start(f32[4,256,768]{2,1,0:T(8,128)} %copy-done.4) | copy-start | bytes 9437188
  535.7 33.2 %copy-start.11 = (bf16[4,256,768]{2,1,0:T(8,128)(2,1)S(1)}, bf16[4,256,768]{2,1,0:T(8,128)(2,1)}, u32[]{:S(2)}) copy-start(bf16[4,256,768]{2,1,0:T(8,128)(2,1)} %copy.56) | copy-start | bytes 4718596
  535.7 33.2 %copy-start.15 = (f32[4,256]{1,0:T(4,128)S(1)}, f32[4,256]{1,0:T(4,128)}, u32[]{:S(2)}) copy-start(f32[4,256]{1,0:T(4,128)} %copy-done.14) | copy-start | bytes 12292
  535.8 33.2 %copy-start.20 = (f32[4,256]{1,0:T(4,128)S(1)}, f32[4,256]{1,0:T(4,128)}, u32[]{:S(2)}) copy-start(f32[4,256]{1,0:T(4,128)} %copy-done.19) | copy-start | bytes 12292
  535.8 33.2 %copy-start.35 = (f32[768]{0:T(1024)S(1)}, f32[768]{0:T(1024)}, u32[]{:S(2)}) copy-start(f32[768]{0:T(1024)} %param.25) | copy-start | bytes 9220
  (27 other events, 108.7 us)
Sparse Core Ops, SparseCore 0:
  578.8 67.5 all-gather.3
